TPU v7x, 32 devices: a whole 2x2x4 slice. The times are simulated.
32 devices in a mesh: fsdp: 4 (over x, core), tm: 8 (over z, y).
Axes of the slice: x: 2, y: 2, z: 4, core: 2. Of those that a mesh axis runs over, the one named last changes fastest.
Arguments:
- tokens: bfloat16 [8, 8, 256, 1024], P('fsdp', 'tm'), may hold values from -6 to 6
- spatial_gain: float32 [1024], replicated, may hold values from 0.25 to 1.75
- spatial_qkv: bfloat16 [1024, 1536], P('fsdp'), may hold values from -16 to 16
- spatial_out: bfloat16 [512, 1024], P('fsdp'), may hold values from -0.25 to 0.25
- temporal_gain: float32 [1024], replicated, may hold values from 0.25 to 1.75
- temporal_qkv: bfloat16 [1024, 1536], P('fsdp'), may hold values from -16 to 16
- temporal_out: bfloat16 [512, 1024], P('fsdp'), may hold values from -0.25 to 0.25
Outputs:
- encoded: bfloat16 [8, 8, 256, 1024], P('fsdp', 'tm')
All inputs are finite; a program needn't handle non-finite values.
Results may differ from a plain program's by a relative error of at most 0.0061.
Values may be sent and summed in bfloat16 or wider, within the bound.
A program may use at most 64 MiB of HBM per device.

v0:
```python
import functools

import jax
import jax.numpy as jnp
from jax import lax
from jax.experimental import pallas as pl
from jax.experimental.pallas import tpu as pltpu
from jax.sharding import PartitionSpec as P

HEAD = 64
LANES = 128
EPSILON = 1e-06
MESH = pl.DeviceIdType.MESH
BF16 = jnp.bfloat16
F32 = jnp.float32


def pieces_of(depth):
    return max(2, depth // 32)


def kernel(
    n_f, n_t, tok, sg, sqkv, sout, tg, tqkv, tout, out,
    xv, normed, proj, ctx, mid, arrived, ctx_t, ctx_back, wsq, wso, wtq, wto, outv,
    local_sem, w_local, w_send, w_recv, m_send, m_recv, o_send, o_recv,
    a_send, a_recv, c_send, c_recv, own_sem, out_sem,
):
    f = lax.axis_index("fsdp")
    t = lax.axis_index("tm")
    mate = f + 1 - 2 * (f % 2)
    peers = n_f // 2 - 1
    clips = xv.shape[0]
    rows, width = xv.shape[1:]
    places = rows // n_t
    inner = wso.shape[0]

    barrier = pltpu.get_barrier_semaphore()
    pl.semaphore_signal(barrier, inc=1, device_id={"fsdp": mate}, device_id_type=MESH)
    for k in range(1, peers + 1):
        pl.semaphore_signal(
            barrier, inc=1, device_id={"fsdp": (f + 2 * k) % n_f}, device_id_type=MESH
        )
    for j in range(1, n_t):
        pl.semaphore_signal(
            barrier, inc=1, device_id={"tm": (t + j) % n_t}, device_id_type=MESH
        )

    token_copy = pltpu.make_async_copy(tok, xv, local_sem)
    token_copy.start()
    weights = ((sqkv, wsq), (sout, wso), (tqkv, wtq), (tout, wto))
    own_weights = []
    for w, (src, dst) in enumerate(weights):
        depth = src.shape[0]
        cp = pltpu.make_async_copy(src, dst.at[pl.ds(f * depth, depth)], w_local.at[w])
        cp.start()
        own_weights.append(cp)

    pl.semaphore_wait(barrier, 1 + peers + n_t - 1)

    sends = []

    def peer_copy(w, k, p, source):
        src, dst = weights[w]
        depth = src.shape[0]
        size = depth // pieces_of(depth)
        return pltpu.make_async_remote_copy(
            src_ref=src.at[pl.ds(p * size, size)],
            dst_ref=dst.at[pl.ds(pl.multiple_of(source * depth + p * size, size), size)],
            send_sem=w_send.at[w, k, p],
            recv_sem=w_recv.at[w, k, p],
            device_id={"fsdp": (f + 2 * (k + 1)) % n_f},
            device_id_type=MESH,
        )

    def mate_own(w, source):
        src, dst = weights[w]
        depth = src.shape[0]
        return pltpu.make_async_remote_copy(
            src_ref=src,
            dst_ref=dst.at[pl.ds(pl.multiple_of(source * depth, depth), depth)],
            send_sem=o_send.at[w],
            recv_sem=o_recv.at[w],
            device_id={"fsdp": mate},
            device_id_type=MESH,
        )

    def mate_forward(w, k, p, source):
        src, dst = weights[w]
        depth = src.shape[0]
        size = depth // pieces_of(depth)
        where = pl.ds(pl.multiple_of(source * depth + p * size, size), size)
        return pltpu.make_async_remote_copy(
            src_ref=dst.at[where],
            dst_ref=dst.at[where],
            send_sem=m_send.at[w, k, p],
            recv_sem=m_recv.at[w, k, p],
            device_id={"fsdp": mate},
            device_id_type=MESH,
        )

    parity = t % 2
    partner = t + 1 - 2 * parity
    half = pieces_of(sqkv.shape[0]) // 2
    small = sqkv.shape[0] // pieces_of(sqkv.shape[0])

    def half_rows(source, part, i):
        start = source * sqkv.shape[0] + (part * half + i) * small
        return pl.ds(pl.multiple_of(start, small), small)

    def direct(k, i, source):
        return pltpu.make_async_remote_copy(
            src_ref=sqkv.at[pl.ds(pl.multiple_of((parity * half + i) * small, small), small)],
            dst_ref=wsq.at[half_rows(source, parity, i)],
            send_sem=w_send.at[0, k, i],
            recv_sem=w_recv.at[0, k, i],
            device_id={"fsdp": (f + 2 * (k + 1)) % n_f},
            device_id_type=MESH,
        )

    def cross(k, i, source, part):
        return pltpu.make_async_remote_copy(
            src_ref=wsq.at[half_rows(source, part, i)],
            dst_ref=wsq.at[half_rows(source, part, i)],
            send_sem=w_send.at[0, k, half + i],
            recv_sem=w_recv.at[0, k, half + i],
            device_id={"tm": partner},
            device_id_type=MESH,
        )

    def half_forward(k, i, source, part, slot):
        return pltpu.make_async_remote_copy(
            src_ref=wsq.at[half_rows(source, part, i)],
            dst_ref=wsq.at[half_rows(source, part, i)],
            send_sem=m_send.at[0, k, slot],
            recv_sem=m_recv.at[0, k, slot],
            device_id={"fsdp": mate},
            device_id_type=MESH,
        )

    def source_of(who, k):
        return (who + n_f - 2 * (k + 1)) % n_f

    def relay_first():
        for i in range(half + 1):
            for k in range(peers):
                source = source_of(f, k)
                if i < half:
                    direct(k, i, source).wait_recv()
                    for cp in (
                        cross(k, i, source, parity),
                        half_forward(k, i, source, parity, i),
                    ):
                        cp.start()
                        sends.append(cp)
                if i > 0:
                    cross(k, i - 1, source, 1 - parity).wait_recv()
                    cp = half_forward(k, i - 1, source, 1 - parity, half + i - 1)
                    cp.start()
                    sends.append(cp)

    def gathered_first():
        own_weights[0].wait()
        mate_own(0, mate).wait_recv()
        for i in range(half):
            for k in range(peers):
                source = source_of(mate, k)
                half_forward(k, i, source, parity, i).wait_recv()
                half_forward(k, i, source, 1 - parity, half + i).wait_recv()

    for w, (src, dst) in enumerate(weights):
        for p in range(half if w == 0 else pieces_of(src.shape[0])):
            for k in range(peers):
                cp = direct(k, p, f) if w == 0 else peer_copy(w, k, p, f)
                cp.start()
                sends.append(cp)
        cp = mate_own(w, f)
        cp.start()
        sends.append(cp)

    def relay(w):
        for p in range(pieces_of(weights[w][0].shape[0])):
            for k in range(peers):
                source = (f + n_f - 2 * (k + 1)) % n_f
                peer_copy(w, k, p, source).wait_recv()
                cp = mate_forward(w, k, p, source)
                cp.start()
                sends.append(cp)

    def gathered(w):
        own_weights[w].wait()
        mate_own(w, mate).wait_recv()
        for p in range(pieces_of(weights[w][0].shape[0])):
            for k in range(peers):
                mate_forward(w, k, p, (mate + n_f - 2 * (k + 1)) % n_f).wait_recv()

    def norm(values, gain):
        centre = values - jnp.mean(values, axis=-1, keepdims=True)
        spread = jnp.mean(centre * centre, axis=-1, keepdims=True)
        return (centre * lax.rsqrt(spread + EPSILON) * gain).astype(BF16)

    def project(c, weight):
        tile = inner

        @pl.loop(0, weight.shape[1] // tile)
        def _(i):
            cols = pl.ds(pl.multiple_of(i * tile, LANES), tile)
            part = jnp.dot(normed[c], weight[:, cols], preferred_element_type=F32)
            proj[c, :, :, cols] = part.reshape(n_t, places, tile)

    def attend(c, lo, group, count, masked, store):
        size = n_t * group
        lane = lax.broadcasted_iota(jnp.int32, (1, LANES), 1)
        first = lane < HEAD

        if masked:
            r = lax.rem(lax.broadcasted_iota(jnp.int32, (size, 1), 0), group)
            l = lax.rem(lax.broadcasted_iota(jnp.int32, (1, size), 1), group)
            same_place = r == l

        @pl.loop(0, inner // LANES, unroll=2)
        def _(i):
            def read(offset):
                cols = pl.ds(pl.multiple_of(offset + i * LANES, LANES), LANES)
                return proj[c, :, lo : lo + group, cols].reshape(size, LANES)

            q = read(0) * HEAD ** (-0.5)
            k = read(inner)
            v = read(2 * inner).astype(BF16)
            kh = k.astype(BF16)
            kl = (k - kh.astype(F32)).astype(BF16)
            kk = jnp.concatenate([kh, kh], axis=1)
            parts = []
            for h in range(LANES // HEAD):
                qm = jnp.where(first == (h == 0), q, 0.0)
                qh = qm.astype(BF16)
                ql = (qm - qh.astype(F32)).astype(BF16)
                qq = jnp.concatenate([qh, ql], axis=1)
                dims = (((1,), (1,)), ((), ()))
                s = lax.dot_general(qq, kk, dims, preferred_element_type=F32)
                s = s + lax.dot_general(qh, kl, dims, preferred_element_type=F32)
                if masked:
                    s = jnp.where(same_place, s, -1e30)
                e = jnp.exp(s - jnp.max(s, axis=-1, keepdims=True))
                total = jnp.sum(e, axis=-1, keepdims=True)
                pv = jnp.dot(e.astype(BF16), v, preferred_element_type=F32)
                parts.append(pv / total)
            result = jnp.where(first, parts[0], parts[1])
            store(pl.ds(pl.multiple_of(i * LANES, LANES), LANES), result)

    def a2a(c, j, slot_from, send):
        to = (t + j) % n_t
        return pltpu.make_async_remote_copy(
            src_ref=mid.at[c, to],
            dst_ref=arrived.at[c, slot_from],
            send_sem=a_send.at[c, j],
            recv_sem=a_recv.at[c, j],
            device_id={"tm": to},
            device_id_type=MESH,
        )

    def back(c, j, slot_from):
        to = (t + j) % n_t
        return pltpu.make_async_remote_copy(
            src_ref=ctx_t.at[c, to],
            dst_ref=ctx_back.at[c, slot_from],
            send_sem=c_send.at[c, j],
            recv_sem=c_recv.at[c, j],
            device_id={"tm": to},
            device_id_type=MESH,
        )

    token_copy.wait()
    block = min(rows, 64)
    for c in range(clips):

        @pl.loop(0, rows // block)
        def _(i):
            where = pl.ds(pl.multiple_of(i * block, block), block)
            normed[c, where] = norm(xv[c, where].astype(F32), sg[...])

    relay_first()
    gathered_first()
    for c in range(clips):
        project(c, wsq)
    own_copies = []
    for c in range(clips):

        def store_spatial(cols, result):
            ctx[:, cols] = result.astype(BF16)

        attend(c, 0, places, 1, False, store_spatial)
        if c == 0:
            relay(1)
            gathered(1)

        @pl.loop(0, width // inner)
        def _(i):
            cols = pl.ds(pl.multiple_of(i * inner, LANES), inner)
            part = xv[c, :, cols].astype(F32) + jnp.dot(
                ctx[...], wso[:, cols], preferred_element_type=F32
            )
            mid[c, :, :, cols] = part.reshape(n_t, places, inner).astype(BF16)

        for j in range(1, n_t):
            cp = a2a(c, j, t, True)
            cp.start()
            sends.append(cp)
        cp = pltpu.make_async_copy(mid.at[c, t], arrived.at[c, t], own_sem.at[0, c])
        cp.start()
        own_copies.append(cp)

    relay(2)
    own_back = []
    group = min(places, 16)
    for c in range(clips):
        own_copies[c].wait()
        for j in range(1, n_t):
            a2a(c, j, (t + n_t - j) % n_t, False).wait_recv()
        step = max(1, block // places)

        @pl.loop(0, n_t // step)
        def _(i):
            values = arrived[c, pl.ds(i * step, step)].astype(F32).reshape(step * places, width)
            where = pl.ds(pl.multiple_of(i * step * places, step * places), step * places)
            normed[c, where] = norm(values, tg[...])

        if c == 0:
            gathered(2)
        project(c, wtq)
        for g in range(places // group):

            def store_temporal(cols, result):
                ctx_t[c, :, g * group : (g + 1) * group, cols] = result.reshape(
                    n_t, group, LANES
                ).astype(BF16)

            attend(c, g * group, group, n_t, True, store_temporal)
        for j in range(1, n_t):
            cp = back(c, j, t)
            cp.start()
            sends.append(cp)
        cp = pltpu.make_async_copy(ctx_t.at[c, t], ctx_back.at[c, t], own_sem.at[1, c])
        cp.start()
        own_back.append(cp)
        if c == 0:
            relay(3)
    gathered(3)
    finals = []
    for c in range(clips):
        own_back[c].wait()
        for j in range(1, n_t):
            back(c, j, (t + n_t - j) % n_t).wait_recv()
        ctx[...] = ctx_back[c].astype(F32).reshape(rows, inner).astype(BF16)

        @pl.loop(0, width // inner)
        def _(i):
            cols = pl.ds(pl.multiple_of(i * inner, LANES), inner)
            part = mid[c, :, :, cols].astype(F32).reshape(rows, inner) + jnp.dot(
                ctx[...], wto[:, cols], preferred_element_type=F32
            )
            outv[c, :, cols] = part.astype(BF16)

        cp = pltpu.make_async_copy(outv.at[c], out.at[c], out_sem.at[c])
        cp.start()
        finals.append(cp)
    for cp in sends:
        cp.wait_send()
    for cp in finals:
        cp.wait()


def shards(
    n_f, n_t, tokens, spatial_gain, spatial_qkv, spatial_out, temporal_gain, temporal_qkv,
    temporal_out,
):
    clip_count, frames, rows, width = tokens.shape
    assert frames == 1
    inner = spatial_out.shape[0] * n_f
    columns = spatial_qkv.shape[1]
    places = rows // n_t
    peers = max(1, n_f // 2 - 1)
    most = pieces_of(max(spatial_qkv.shape[0], spatial_out.shape[0]))
    anywhere = pl.BlockSpec(memory_space=pl.ANY)
    vmem = pl.BlockSpec(memory_space=pltpu.VMEM)
    dma = pltpu.SemaphoreType.DMA
    result = pl.pallas_call(
        functools.partial(kernel, n_f, n_t),
        out_shape=jax.ShapeDtypeStruct((clip_count, rows, width), BF16),
        in_specs=[anywhere, vmem, anywhere, anywhere, vmem, anywhere, anywhere],
        out_specs=anywhere,
        scratch_shapes=[
            pltpu.VMEM((clip_count, rows, width), BF16),
            pltpu.VMEM((clip_count, rows, width), BF16),
            pltpu.VMEM((clip_count, n_t, places, columns), F32),
            pltpu.VMEM((rows, inner), BF16),
            pltpu.VMEM((clip_count, n_t, places, width), BF16),
            pltpu.VMEM((clip_count, n_t, places, width), BF16),
            pltpu.VMEM((clip_count, n_t, places, inner), BF16),
            pltpu.VMEM((clip_count, n_t, places, inner), BF16),
            pltpu.VMEM((width, columns), BF16),
            pltpu.VMEM((inner, width), BF16),
            pltpu.VMEM((width, columns), BF16),
            pltpu.VMEM((inner, width), BF16),
            pltpu.VMEM((clip_count, rows, width), BF16),
            dma,
            dma((4,)),
            dma((4, peers, most)),
            dma((4, peers, most)),
            dma((4, peers, most)),
            dma((4, peers, most)),
            dma((4,)),
            dma((4,)),
            dma((clip_count, n_t)),
            dma((clip_count, n_t)),
            dma((clip_count, n_t)),
            dma((clip_count, n_t)),
            dma((2, clip_count)),
            dma((clip_count,)),
        ],
        compiler_params=pltpu.CompilerParams(
            collective_id=0, has_side_effects=True, vmem_limit_bytes=67000000
        ),
    )(
        tokens.reshape(clip_count, rows, width),
        spatial_gain.reshape(1, width),
        spatial_qkv,
        spatial_out,
        temporal_gain.reshape(1, width),
        temporal_qkv,
        temporal_out,
    )
    return result.reshape(clip_count, frames, rows, width)


def solution(mesh):
    placed = (
        P("fsdp", "tm", None, None),
        P(),
        P("fsdp", None),
        P("fsdp", None),
        P(),
        P("fsdp", None),
        P("fsdp", None),
    )
    body = functools.partial(shards, mesh.shape["fsdp"], mesh.shape["tm"])
    return jax.shard_map(
        body, mesh=mesh, in_specs=placed, out_specs=P("fsdp", "tm", None, None), check_vma=False
    )
```

profile of v0, /device:TPU:0, one launch (start us, length us, event | category | flops | bytes accessed | tf_op | source)
XLA Modules:
  0.0 74.5 jit_solution(14066856075550617031)
XLA Ops:
  0.0 72.3 %shard_map.73 = bf16[2,256,1024]{2,1,0:T(8,128)(2,1)} custom-call(bf16[2,256,1024]{2,1,0:T(8,128)(2,1)} %bitcast.7, f32[1,1024]{1,0:T(1,128)} %bitcast.8, bf16[256,1536]{1,0:T(8,128)(2,1)} %sqkv.1, bf16[128,1024]{1,0:T(8,128)(2,1)} %sout.1, f32[1,1024]{1,0:T(1,128)} %bitcast.9, bf16[256,1536]{1,0:T(8,128)(2,1)} %tqkv.1, bf16[128,1024]{1,0:T(8,128)(2,1)} %tout.1), custom_call_target="tpu_custom_call" | custom-call | tf_op jit(solution)/shard_map/pallas_call | solution.py:386
  72.3 2.3 %copy.10 = bf16[2,1,256,1024]{3,2,1,0:T(8,128)(2,1)} copy(bf16[2,1,256,1024]{3,2,1,0:T(8,128)(2,1)} %bitcast.6) | data formatting | bytes 2097152
where the time goes:
time: 74.7 us; the launch traced here: 74.5 us
  Pallas kernels  72.3 us (97%)
  local copies, waits for them, and re-layouts  2.26 us (3%)
    pallas_call x1, Pallas kernels, shards(): pl.pallas_call(functools.partial(kernel, n_f, n_t), out_shape=jax.ShapeDt...  72.3 us
    unnamed x1, local copies, waits for them, and re-layouts  2.26 us

commit v1 on v0

v1 whole, which is shorter than its diff:
```python
import functools

import jax
import jax.numpy as jnp
from jax import lax
from jax.experimental import pallas as pl
from jax.experimental.pallas import tpu as pltpu
from jax.sharding import PartitionSpec as P

HEAD = 64
LANES = 128
EPSILON = 1e-06
MESH = pl.DeviceIdType.MESH
BF16 = jnp.bfloat16
F32 = jnp.float32


def pieces_of(depth):
    return max(2, depth // 32)


def crossed_of(w, depth):
    count = pieces_of(depth)
    return (count // 2, count // 2, count // 4, 0)[w]


def kernel(
    n_f, n_t, tok, sg, sqkv, sout, tg, tqkv, tout, out,
    xv, normed, proj, ctx, mid, arrived, normed_t, proj_t, ctx_t, ctx_back,
    wsq, wso, wtq, wto, outv,
    ack, ack_t, local_sem, w_local, w_send, w_recv, y_send, y_recv, m_send, m_recv, o_send, o_recv,
    p_send, p_recv, a_send, a_recv, c_send, c_recv, own_sem, out_sem,
):
    f = lax.axis_index("fsdp")
    t = lax.axis_index("tm")
    core = f % 2
    mate = f + 1 - 2 * core
    peers = n_f // 2 - 1
    half = n_t // 2
    side = t // half
    u = t % half
    partner = (t + half) % n_t
    keep = xv.shape[0] // 3
    rows, width = xv.shape[1:]
    inner = wso.shape[0]
    places = rows // half
    sends = []

    def start(cp):
        cp.start()
        sends.append(cp)

    barrier = pltpu.get_barrier_semaphore()
    for j in range(1, n_t):

        @pl.when(t + j < n_t)
        def _():
            pl.semaphore_signal(
                barrier, inc=1, device_id={"tm": (t + j) % n_t}, device_id_type=MESH
            )

    @pl.when(core == 0)
    def _():
        pl.semaphore_signal(barrier, inc=1, device_id={"fsdp": mate}, device_id_type=MESH)

    for k in range(peers):

        @pl.when(f + 2 * (k + 1) < n_f)
        def _():
            pl.semaphore_signal(
                barrier,
                inc=1,
                device_id={"fsdp": (f + 2 * (k + 1)) % n_f},
                device_id_type=MESH,
            )

    token_copies = []
    for c in range(keep):
        for slot, src in ((c, side * keep + c), (2 * keep + c, (1 - side) * keep + c)):
            cp = pltpu.make_async_copy(tok.at[src], xv.at[slot], local_sem.at[slot])
            cp.start()
            token_copies.append(cp)
    weights = ((sqkv, wsq), (sout, wso), (tqkv, wtq), (tout, wto))
    own_weights = []
    for w, (src, dst) in enumerate(weights):
        depth = src.shape[0]
        cp = pltpu.make_async_copy(src, dst.at[pl.ds(f * depth, depth)], w_local.at[w])
        cp.start()
        own_weights.append(cp)

    lower = t + core + f // 2

    @pl.when(lower > 0)
    def _():
        pl.semaphore_wait(barrier, lower)


    @pl.when(core == 1)
    def _():
        pl.semaphore_signal(ack.at[peers], inc=1, device_id={"fsdp": mate}, device_id_type=MESH)

    def source_of(who, k):
        return (who + n_f - 2 * (k + 1)) % n_f

    for k in range(peers):

        @pl.when(f >= 2 * (k + 1))
        def _():
            pl.semaphore_signal(
                ack.at[k], inc=1, device_id={"fsdp": source_of(f, k)}, device_id_type=MESH
            )

    for j in range(1, n_t):

        @pl.when(t >= j)
        def _():
            pl.semaphore_signal(
                ack_t.at[j], inc=1, device_id={"tm": (t + n_t - j) % n_t}, device_id_type=MESH
            )

    def entered(condition, j):
        @pl.when(condition)
        def _():
            pl.semaphore_wait(ack_t.at[j], 1)

    parity = t % 2
    beside = t + 1 - 2 * parity

    def rows_of(w, source, i, par):
        depth = weights[w][0].shape[0]
        count = pieces_of(depth)
        size = depth // count
        piece = i + par * (count - 1 - 2 * i)
        return pl.ds(pl.multiple_of(source * depth + piece * size, size), size)

    def direct(w, k, i, source):
        src, dst = weights[w]
        return pltpu.make_async_remote_copy(
            src_ref=src.at[rows_of(w, 0, i, parity)],
            dst_ref=dst.at[rows_of(w, source, i, parity)],
            send_sem=w_send.at[w, k, i],
            recv_sem=w_recv.at[w, k, i],
            device_id={"fsdp": (f + 2 * (k + 1)) % n_f},
            device_id_type=MESH,
        )

    def cross(w, k, i, source, par):
        dst = weights[w][1]
        where = rows_of(w, source, i, par)
        return pltpu.make_async_remote_copy(
            src_ref=dst.at[where],
            dst_ref=dst.at[where],
            send_sem=y_send.at[w, k, i],
            recv_sem=y_recv.at[w, k, i],
            device_id={"tm": beside},
            device_id_type=MESH,
        )

    def forward(w, k, i, source, par, slot):
        dst = weights[w][1]
        where = rows_of(w, source, i, par)
        return pltpu.make_async_remote_copy(
            src_ref=dst.at[where],
            dst_ref=dst.at[where],
            send_sem=m_send.at[w, k, slot],
            recv_sem=m_recv.at[w, k, slot],
            device_id={"fsdp": mate},
            device_id_type=MESH,
        )

    def mate_own(w, source):
        src, dst = weights[w]
        depth = src.shape[0]
        return pltpu.make_async_remote_copy(
            src_ref=src,
            dst_ref=dst.at[pl.ds(pl.multiple_of(source * depth, depth), depth)],
            send_sem=o_send.at[w],
            recv_sem=o_recv.at[w],
            device_id={"fsdp": mate},
            device_id_type=MESH,
        )

    def counts(w):
        depth = weights[w][0].shape[0]
        crossed = crossed_of(w, depth)
        return pieces_of(depth) - crossed, crossed

    def send_direct(w):
        for i in range(counts(w)[0]):
            for k in range(peers):
                start(direct(w, k, i, f))

    def relay(w, lo=0, hi=None):
        straight, crossed = counts(w)
        for i in range(lo, straight if hi is None else hi):
            for k in range(peers):
                source = source_of(f, k)
                direct(w, k, i, source).wait_recv()
                if i < crossed:
                    start(cross(w, k, i, source, parity))
                start(forward(w, k, i, source, parity, i))
        if hi is None:
            for i in range(crossed):
                for k in range(peers):
                    source = source_of(f, k)
                    cross(w, k, i, source, 1 - parity).wait_recv()
                    start(forward(w, k, i, source, 1 - parity, straight + i))

    def gathered(w):
        straight, crossed = counts(w)
        own_weights[w].wait()
        mate_own(w, mate).wait_recv()
        for k in range(peers):
            source = source_of(mate, k)
            for i in range(straight):
                forward(w, k, i, source, parity, i).wait_recv()
            for i in range(crossed):
                forward(w, k, i, source, 1 - parity, straight + i).wait_recv()

    def presend(c):
        return pltpu.make_async_remote_copy(
            src_ref=tok.at[(1 - side) * keep + c],
            dst_ref=xv.at[keep + c],
            send_sem=p_send.at[c],
            recv_sem=p_recv.at[c],
            device_id={"tm": partner},
            device_id_type=MESH,
        )

    def norm(values, gain):
        centre = values - jnp.mean(values, axis=-1, keepdims=True)
        spread = jnp.mean(centre * centre, axis=-1, keepdims=True)
        return (centre * lax.rsqrt(spread + EPSILON) * gain).astype(BF16)

    block = min(rows, 64)

    def norm_spatial(job):
        @pl.loop(0, rows // block)
        def _(i):
            where = pl.ds(pl.multiple_of(i * block, block), block)
            normed[job, where] = norm(xv[job, where].astype(F32), sg[...])

    def attend(read, size, same_place, store):
        lane = lax.broadcasted_iota(jnp.int32, (1, LANES), 1)
        first = lane < HEAD
        dims = (((1,), (1,)), ((), ()))

        @pl.loop(0, inner // LANES, unroll=4)
        def _(i):
            def load(offset):
                return read(pl.ds(pl.multiple_of(offset + i * LANES, LANES), LANES))

            q = load(0) * HEAD ** (-0.5)
            k = load(inner)
            v = load(2 * inner)
            qh = q.astype(BF16).astype(F32)
            ql = pltpu.roll(q - qh, HEAD, 1)
            kh = k.astype(BF16).astype(F32)
            kl = (k - kh).astype(BF16)
            kr = pltpu.roll(kh, HEAD, 1)
            parts = []
            for own in (first, jnp.logical_not(first)):
                high = jnp.where(own, qh, 0.0).astype(BF16)
                left = jnp.concatenate([jnp.where(own, qh, ql).astype(BF16), high], axis=1)
                right = jnp.concatenate([jnp.where(own, kh, kr).astype(BF16), kl], axis=1)
                s = lax.dot_general(left, right, dims, preferred_element_type=F32)
                if same_place is not None:
                    s = jnp.where(same_place, s, -1e30)
                e = jnp.exp(s - jnp.max(s, axis=-1, keepdims=True)).astype(BF16)
                ones = jnp.where(own, v, 1.0).astype(BF16)
                parts.append(jnp.dot(e, ones, preferred_element_type=F32))
            total = pltpu.roll(jnp.where(first, parts[1], parts[0]), HEAD, 1)
            result = jnp.where(first, parts[0], parts[1]) / total
            store(pl.ds(pl.multiple_of(i * LANES, LANES), LANES), result)

    def a2a(kind, c, j, to, frame):
        return pltpu.make_async_remote_copy(
            src_ref=mid.at[kind * keep + c, to % half],
            dst_ref=arrived.at[c, frame],
            send_sem=a_send.at[kind, c, j],
            recv_sem=a_recv.at[kind, c, j],
            device_id={"tm": to},
            device_id_type=MESH,
        )

    def own_mid(kind, c):
        frame = t if kind == 0 else partner
        return pltpu.make_async_copy(
            mid.at[kind * keep + c, u], arrived.at[c, frame], own_sem.at[kind, c]
        )

    def within(j):
        return side * half + (u + j) % half

    def send_mid(kind, c):
        for j in range(1, half):
            a2a(kind, c, j, within(j), t if kind == 0 else partner).start()
        own_mid(kind, c).start()

    def spatial(job):
        @pl.loop(0, 3)
        def _(i):
            cols = pl.ds(pl.multiple_of(i * inner, LANES), inner)
            proj[:, cols] = jnp.dot(normed[job], wsq[:, cols], preferred_element_type=F32)

        def store(cols, result):
            ctx[:, cols] = result.astype(BF16)

        attend(lambda cols: proj[:, cols], rows, None, store)

    def spatial_out(job):
        @pl.loop(0, width // inner)
        def _(i):
            cols = pl.ds(pl.multiple_of(i * inner, LANES), inner)
            part = xv[job, :, cols].astype(F32) + jnp.dot(
                ctx[...], wso[:, cols], preferred_element_type=F32
            )
            mid[job, :, :, cols] = part.reshape(half, places, inner).astype(BF16)

    @pl.when(core == 1)
    def _():
        for w in range(4):
            mate_own(w, f).start()

    for k in range(peers):

        @pl.when(f + 2 * (k + 1) < n_f)
        def _():
            pl.semaphore_wait(ack.at[k], 1)

    for w in range(4):
        send_direct(w)
    for cp in token_copies:
        cp.wait()
    for c in range(keep):
        norm_spatial(c)

    @pl.when(core == 0)
    def _():
        pl.semaphore_wait(ack.at[peers], 1)
        for w in range(4):
            mate_own(w, f).start()

    entered(t < half, half)

    @pl.when(core == 0)
    def _():
        for c in range(keep):
            presend(c).start()

    entered(parity == 0, 1)
    for c in range(keep):
        norm_spatial(2 * keep + c)

    relay(0)
    gathered(0)

    @pl.when(core == 1)
    def _():
        for c in range(keep):
            presend(c).start()

    for j in range(1, half):
        entered((u + j < half) & ((parity == 1) | (j > 1)), j)
    for c in range(keep):
        spatial(c)
        if c == 0:
            relay(1)
            gathered(1)
        spatial_out(c)
        send_mid(0, c)

    straight = counts(2)[0]
    relay(2, 0, straight // 3)

    def foreign(c):
        presend(c).wait_recv()
        norm_spatial(keep + c)

    for step in range(2):
        for c in range(keep):
            kind = 1 + core if step == 0 else 2 - core
            job = kind * keep + c

            @pl.when(kind == 1)
            def _():
                foreign(c)

            spatial(job)
            spatial_out(job)

            @pl.when(kind == 1)
            def _():
                send_mid(1, c)

        if step == 0:
            relay(2, straight // 3, 2 * straight // 3)
    relay(2, 2 * straight // 3)

    steps = max(1, places // 32)
    chunk = places // steps
    group = min(chunk, max(8, LANES // n_t))
    size = n_t * group
    r = lax.rem(lax.broadcasted_iota(jnp.int32, (size, 1), 0), group)
    l = lax.rem(lax.broadcasted_iota(jnp.int32, (1, size), 1), group)
    same_place = r == l

    def back(c, s, j, to, clip, slot):
        lo = s * chunk
        return pltpu.make_async_remote_copy(
            src_ref=ctx_t.at[c, to, pl.ds(lo, chunk)],
            dst_ref=ctx_back.at[clip, slot, pl.ds(lo, chunk)],
            send_sem=c_send.at[c, s, j],
            recv_sem=c_recv.at[c, s, j],
            device_id={"tm": to},
            device_id_type=MESH,
        )

    def own_back(c, s):
        lo = s * chunk
        return pltpu.make_async_copy(
            ctx_t.at[c, t, pl.ds(lo, chunk)],
            ctx_back.at[side * keep + c, u, pl.ds(lo, chunk)],
            own_sem.at[2 + s, c],
        )

    for j in range(1, n_t):
        if j != half:
            entered((t + j < n_t) & (u + j >= half), j)
    far_first = sorted(range(1, n_t), key=lambda j: abs(j - half))
    for c in range(keep):
        for kind in range(2):
            own_mid(kind, c).wait()
            for j in range(1, half):
                source = within(half - j)
                frame = source if kind == 0 else (source + half) % n_t
                a2a(kind, c, j, within(j), frame).wait_recv()
        for s in range(steps):
            lo = s * chunk
            span = max(1, block // chunk)

            @pl.loop(0, n_t // span)
            def _(i):
                frames = pl.ds(i * span, span)
                values = arrived[c, frames, lo : lo + chunk].astype(F32)
                values = norm(values.reshape(span * chunk, width), tg[...])
                where = pl.ds(pl.multiple_of(i * span * chunk, span * chunk), span * chunk)
                normed_t[where] = values

            if c == 0 and s == 0:
                gathered(2)

            @pl.loop(0, 3)
            def _(i):
                cols = pl.ds(pl.multiple_of(i * inner, LANES), inner)
                part = jnp.dot(normed_t[...], wtq[:, cols], preferred_element_type=F32)
                proj_t[:, :, cols] = part.reshape(n_t, chunk, inner)

            for g in range(chunk // group):
                at = g * group

                def store(cols, result):
                    ctx_t[c, :, lo + at : lo + at + group, cols] = result.reshape(
                        n_t, group, LANES
                    ).astype(BF16)

                attend(
                    lambda cols: proj_t[:, at : at + group, cols].reshape(size, LANES),
                    size, same_place, store,
                )
            for j in far_first:
                start(back(c, s, j, (t + j) % n_t, side * keep + c, u))
            own_back(c, s).start()
    relay(3)
    gathered(3)

    finals = []
    for far in (False, True):
        clip_side = 1 - side if far else side
        for c in range(keep):
            clip = clip_side * keep + c
            job = (2 if far else 0) * keep + c
            for s in range(steps):
                lo = s * chunk
                if not far:
                    own_back(c, s).wait()
                for j in range(1, n_t):
                    source = (t + n_t - j) % n_t

                    @pl.when((source // half == side) != far)
                    def _():
                        back(c, s, j, (t + j) % n_t, clip, source % half).wait_recv()

                part_rows = half * chunk
                now = ctx_back[clip, :, lo : lo + chunk].reshape(part_rows, inner)

                @pl.loop(0, width // inner)
                def _(i):
                    cols = pl.ds(pl.multiple_of(i * inner, LANES), inner)
                    base = mid[job, :, lo : lo + chunk, cols].astype(F32)
                    part = base.reshape(part_rows, inner) + jnp.dot(
                        now, wto[:, cols], preferred_element_type=F32
                    )
                    outv[far * keep + c, :, lo : lo + chunk, cols] = part.reshape(
                        half, chunk, inner
                    ).astype(BF16)

            cp = pltpu.make_async_copy(outv.at[far * keep + c], out.at[clip], out_sem.at[far * keep + c])
            cp.start()
            finals.append(cp)

    for c in range(keep):
        presend(c).wait_send()
        for kind in range(2):
            for j in range(1, half):
                a2a(kind, c, j, within(j), t).wait_send()
    for w in range(4):
        mate_own(w, f).wait_send()
    for cp in sends:
        cp.wait_send()
    for cp in finals:
        cp.wait()


def shards(
    n_f, n_t, tokens, spatial_gain, spatial_qkv, spatial_out, temporal_gain, temporal_qkv,
    temporal_out,
):
    clip_count, frames, rows, width = tokens.shape
    assert frames == 1 and clip_count % 2 == 0 and n_t % 4 == 0
    inner = spatial_out.shape[0] * n_f
    columns = spatial_qkv.shape[1]
    keep = clip_count // 2
    half = n_t // 2
    places = rows // half
    steps = max(1, places // 32)
    chunk = places // steps
    peers = max(1, n_f // 2 - 1)
    most = pieces_of(max(spatial_qkv.shape[0], spatial_out.shape[0]))
    anywhere = pl.BlockSpec(memory_space=pl.ANY)
    vmem = pl.BlockSpec(memory_space=pltpu.VMEM)
    dma = pltpu.SemaphoreType.DMA
    result = pl.pallas_call(
        functools.partial(kernel, n_f, n_t),
        out_shape=jax.ShapeDtypeStruct((clip_count, half, places, width), BF16),
        in_specs=[anywhere, vmem, anywhere, anywhere, vmem, anywhere, anywhere],
        out_specs=anywhere,
        scratch_shapes=[
            pltpu.VMEM((3 * keep, rows, width), BF16),
            pltpu.VMEM((3 * keep, rows, width), BF16),
            pltpu.VMEM((rows, columns), F32),
            pltpu.VMEM((rows, inner), BF16),
            pltpu.VMEM((3 * keep, half, places, width), BF16),
            pltpu.VMEM((keep, n_t, places, width), BF16),
            pltpu.VMEM((n_t * chunk, width), BF16),
            pltpu.VMEM((n_t, chunk, columns), F32),
            pltpu.VMEM((keep, n_t, places, inner), BF16),
            pltpu.VMEM((clip_count, half, places, inner), BF16),
            pltpu.VMEM((width, columns), BF16),
            pltpu.VMEM((inner, width), BF16),
            pltpu.VMEM((width, columns), BF16),
            pltpu.VMEM((inner, width), BF16),
            pltpu.VMEM((clip_count, half, places, width), BF16),
            pltpu.SemaphoreType.REGULAR((peers + 1,)),
            pltpu.SemaphoreType.REGULAR((n_t,)),
            dma((3 * keep,)),
            dma((4,)),
            dma((4, peers, most)),
            dma((4, peers, most)),
            dma((4, peers, most)),
            dma((4, peers, most)),
            dma((4, peers, most)),
            dma((4, peers, most)),
            dma((4,)),
            dma((4,)),
            dma((keep,)),
            dma((keep,)),
            dma((2, keep, half)),
            dma((2, keep, half)),
            dma((keep, steps, n_t)),
            dma((keep, steps, n_t)),
            dma((2 + steps, keep)),
            dma((clip_count,)),
        ],
        compiler_params=pltpu.CompilerParams(
            collective_id=0, has_side_effects=True, vmem_limit_bytes=67000000
        ),
    )(
        tokens.reshape(clip_count, rows, width),
        spatial_gain.reshape(1, width),
        spatial_qkv,
        spatial_out,
        temporal_gain.reshape(1, width),
        temporal_qkv,
        temporal_out,
    )
    return result.reshape(clip_count, frames, rows, width)


def solution(mesh):
    placed = (
        P("fsdp", "tm", None, None),
        P(),
        P("fsdp", None),
        P("fsdp", None),
        P(),
        P("fsdp", None),
        P("fsdp", None),
    )
    body = functools.partial(shards, mesh.shape["fsdp"], mesh.shape["tm"])
    return jax.shard_map(
        body, mesh=mesh, in_specs=placed, out_specs=P("fsdp", "tm", None, None), check_vma=False
    )
```

time: 74.7 us -> 70.2 us (0.940)
  Pallas kernels: 72.3 us -> 67.7 us
    pallas_call x1, Pallas kernels: 72.3 us -> 67.7 us  [shards(): pl.pallas_call(functools.partial(kernel, n_f, n_t), out_shape=jax.ShapeDt...]
where the time goes in v1:
time: 70.2 us; the launch traced here: 70 us
  Pallas kernels  67.7 us (96%)
  local copies, waits for them, and re-layouts  2.26 us (3%)
    pallas_call x1, Pallas kernels, shards(): pl.pallas_call(functools.partial(kernel, n_f, n_t), out_shape=jax.ShapeDt...  67.7 us
    unnamed x1, local copies, waits for them, and re-layouts  2.26 us

profile of v1, /device:TPU:0, one launch (start us, length us, event | category | flops | bytes accessed | tf_op | source)
XLA Modules:
  0.0 70.0 jit_solution(13819321615574330564)
XLA Ops:
  0.0 67.7 %shard_map.73 = bf16[2,4,64,1024]{3,2,1,0:T(8,128)(2,1)} custom-call(bf16[2,256,1024]{2,1,0:T(8,128)(2,1)} %bitcast.7, f32[1,1024]{1,0:T(1,128)} %bitcast.8, bf16[256,1536]{1,0:T(8,128)(2,1)} %sqkv.1, bf16[128,1024]{1,0:T(8,128)(2,1)} %sout.1, f32[1,1024]{1,0:T(1,128)} %bitcast.9, bf16[256,1536]{1,0:T(8,128)(2,1)} %tqkv.1, bf16[128,1024]{1,0:T(8,128)(2,1)} %tout.1), custom_call_target="tpu_custom_call" | custom-call | tf_op jit(solution)/shard_map/pallas_call | solution.py:543
  67.7 2.3 %copy.10 = bf16[2,1,256,1024]{3,2,1,0:T(8,128)(2,1)} copy(bf16[2,1,256,1024]{3,2,1,0:T(8,128)(2,1)} %bitcast.6) | data formatting | bytes 2097152

commit v2 on v1

--- a/solution.py
+++ b/solution.py
@@ -16,12 +16,12 @@
 
 
 def pieces_of(depth):
-    return max(2, depth // 32)
+    return max(2, depth // 64)
 
 
 def crossed_of(w, depth):
     count = pieces_of(depth)
-    return (count // 2, count // 2, count // 4, 0)[w]
+    return (count // 2, 0, 0, 0)[w]
 
 
 def kernel(
@@ -40,10 +40,10 @@
     side = t // half
     u = t % half
     partner = (t + half) % n_t
-    keep = xv.shape[0] // 3
+    first_clip = side * (1 - core)
     rows, width = xv.shape[1:]
     inner = wso.shape[0]
-    places = rows // half
+    places = rows // n_t
     sends = []
 
     def start(cp):
@@ -75,11 +75,10 @@
             )
 
     token_copies = []
-    for c in range(keep):
-        for slot, src in ((c, side * keep + c), (2 * keep + c, (1 - side) * keep + c)):
-            cp = pltpu.make_async_copy(tok.at[src], xv.at[slot], local_sem.at[slot])
-            cp.start()
-            token_copies.append(cp)
+    for slot, src in ((0, first_clip), (2, 1 - first_clip)):
+        cp = pltpu.make_async_copy(tok.at[src], xv.at[slot], local_sem.at[slot])
+        cp.start()
+        token_copies.append(cp)
     weights = ((sqkv, wsq), (sout, wso), (tqkv, wtq), (tout, wto))
     own_weights = []
     for w, (src, dst) in enumerate(weights):
@@ -217,12 +216,12 @@
             for i in range(crossed):
                 forward(w, k, i, source, 1 - parity, straight + i).wait_recv()
 
-    def presend(c):
+    def presend():
         return pltpu.make_async_remote_copy(
-            src_ref=tok.at[(1 - side) * keep + c],
-            dst_ref=xv.at[keep + c],
-            send_sem=p_send.at[c],
-            recv_sem=p_recv.at[c],
+            src_ref=tok.at[1 - side],
+            dst_ref=xv.at[1],
+            send_sem=p_send,
+            recv_sem=p_recv,
             device_id={"tm": partner},
             device_id_type=MESH,
         )
@@ -273,29 +272,62 @@
             result = jnp.where(first, parts[0], parts[1]) / total
             store(pl.ds(pl.multiple_of(i * LANES, LANES), LANES), result)
 
-    def a2a(kind, c, j, to, frame):
+    def a2a(kind, s, j, job, to, take, frame):
         return pltpu.make_async_remote_copy(
-            src_ref=mid.at[kind * keep + c, to % half],
-            dst_ref=arrived.at[c, frame],
-            send_sem=a_send.at[kind, c, j],
-            recv_sem=a_recv.at[kind, c, j],
+            src_ref=mid.at[job, take],
+            dst_ref=arrived.at[s, frame],
+            send_sem=a_send.at[kind, s, j],
+            recv_sem=a_recv.at[kind, s, j],
             device_id={"tm": to},
             device_id_type=MESH,
         )
 
-    def own_mid(kind, c):
-        frame = t if kind == 0 else partner
+    def own_mid(kind, s, job, take, frame):
         return pltpu.make_async_copy(
-            mid.at[kind * keep + c, u], arrived.at[c, frame], own_sem.at[kind, c]
-        )
-
-    def within(j):
-        return side * half + (u + j) % half
-
-    def send_mid(kind, c):
-        for j in range(1, half):
-            a2a(kind, c, j, within(j), t if kind == 0 else partner).start()
-        own_mid(kind, c).start()
+            mid.at[job, take], arrived.at[s, frame], own_sem.at[kind, s]
+        )
+
+    far_first = sorted(range(1, n_t), key=lambda j: abs(j - half))
+
+    def near(kind, act):
+        frame = (t, partner)[kind]
+        for s in range(2):
+            for j in range(1, half):
+                there = (u + j) % half
+                act(a2a(kind, s, j, kind, side * half + there, 2 * there + s, frame))
+            if act is begin:
+                own_mid(kind, s, kind, 2 * u + s, frame).start()
+
+    def wide(s, act):
+        job = 2 * s
+        for j in far_first:
+            to = (t + j) % n_t
+            act(a2a(0, s, j, job, to, to, t))
+        if act is begin:
+            own_mid(0, s, job, t, t).start()
+
+    def begin(cp):
+        cp.start()
+
+    def drain(cp):
+        cp.wait_send()
+
+    def arrive(s):
+        @pl.when(core == 0)
+        def _():
+            for kind in range(2):
+                own_mid(kind, s, kind, 2 * u + s, (t, partner)[kind]).wait()
+                for j in range(1, half):
+                    source = side * half + (u + half - j) % half
+                    frame = (source, (source + half) % n_t)[kind]
+                    a2a(kind, s, j, kind, source, 0, frame).wait_recv()
+
+        @pl.when(core == 1)
+        def _():
+            own_mid(0, s, 2 * s, t, t).wait()
+            for j in range(1, n_t):
+                source = (t + n_t - j) % n_t
+                a2a(0, s, j, 2 * s, source, 0, source).wait_recv()
 
     def spatial(job):
         @pl.loop(0, 3)
@@ -315,7 +347,7 @@
             part = xv[job, :, cols].astype(F32) + jnp.dot(
                 ctx[...], wso[:, cols], preferred_element_type=F32
             )
-            mid[job, :, :, cols] = part.reshape(half, places, inner).astype(BF16)
+            mid[job, :, :, cols] = part.reshape(n_t, places, inner).astype(BF16)
 
     @pl.when(core == 1)
     def _():
@@ -330,10 +362,14 @@
 
     for w in range(4):
         send_direct(w)
-    for cp in token_copies:
-        cp.wait()
-    for c in range(keep):
-        norm_spatial(c)
+    entered(t < half, half)
+
+    @pl.when(core == 0)
+    def _():
+        presend().start()
+
+    token_copies[0].wait()
+    norm_spatial(0)
 
     @pl.when(core == 0)
     def _():
@@ -341,183 +377,176 @@
         for w in range(4):
             mate_own(w, f).start()
 
-    entered(t < half, half)
-
-    @pl.when(core == 0)
-    def _():
-        for c in range(keep):
-            presend(c).start()
-
     entered(parity == 0, 1)
-    for c in range(keep):
-        norm_spatial(2 * keep + c)
+    token_copies[1].wait()
+    norm_spatial(2)
 
     relay(0)
     gathered(0)
+    for j in range(1, n_t):
+        if j != half:
+            entered((t + j < n_t) & ((parity == 1) | (j > 1)), j)
+
+    spatial(0)
+    relay(1)
+    gathered(1)
+    spatial_out(0)
+
+    @pl.when(core == 0)
+    def _():
+        near(0, begin)
 
     @pl.when(core == 1)
     def _():
-        for c in range(keep):
-            presend(c).start()
-
-    for j in range(1, half):
-        entered((u + j < half) & ((parity == 1) | (j > 1)), j)
-    for c in range(keep):
-        spatial(c)
-        if c == 0:
-            relay(1)
-            gathered(1)
-        spatial_out(c)
-        send_mid(0, c)
+        wide(0, begin)
 
     straight = counts(2)[0]
     relay(2, 0, straight // 3)
 
-    def foreign(c):
-        presend(c).wait_recv()
-        norm_spatial(keep + c)
-
-    for step in range(2):
-        for c in range(keep):
-            kind = 1 + core if step == 0 else 2 - core
-            job = kind * keep + c
-
-            @pl.when(kind == 1)
-            def _():
-                foreign(c)
-
-            spatial(job)
-            spatial_out(job)
-
-            @pl.when(kind == 1)
-            def _():
-                send_mid(1, c)
-
-        if step == 0:
-            relay(2, straight // 3, 2 * straight // 3)
+    @pl.when(core == 0)
+    def _():
+        presend().wait_recv()
+        norm_spatial(1)
+
+    spatial(1 + core)
+    spatial_out(1 + core)
+
+    @pl.when(core == 0)
+    def _():
+        near(1, begin)
+
+    @pl.when(core == 1)
+    def _():
+        wide(1, begin)
+
+    relay(2, straight // 3, 2 * straight // 3)
+
+    @pl.when(core == 0)
+    def _():
+        spatial(2)
+        spatial_out(2)
+
     relay(2, 2 * straight // 3)
 
-    steps = max(1, places // 32)
-    chunk = places // steps
-    group = min(chunk, max(8, LANES // n_t))
+    group = min(places, max(8, LANES // n_t))
     size = n_t * group
     r = lax.rem(lax.broadcasted_iota(jnp.int32, (size, 1), 0), group)
     l = lax.rem(lax.broadcasted_iota(jnp.int32, (1, size), 1), group)
     same_place = r == l
 
-    def back(c, s, j, to, clip, slot):
-        lo = s * chunk
+    def back(s, j, to, clip, slot):
         return pltpu.make_async_remote_copy(
-            src_ref=ctx_t.at[c, to, pl.ds(lo, chunk)],
-            dst_ref=ctx_back.at[clip, slot, pl.ds(lo, chunk)],
-            send_sem=c_send.at[c, s, j],
-            recv_sem=c_recv.at[c, s, j],
+            src_ref=ctx_t.at[s, to],
+            dst_ref=ctx_back.at[clip, slot],
+            send_sem=c_send.at[s, j],
+            recv_sem=c_recv.at[s, j],
             device_id={"tm": to},
             device_id_type=MESH,
         )
 
-    def own_back(c, s):
-        lo = s * chunk
-        return pltpu.make_async_copy(
-            ctx_t.at[c, t, pl.ds(lo, chunk)],
-            ctx_back.at[side * keep + c, u, pl.ds(lo, chunk)],
-            own_sem.at[2 + s, c],
-        )
-
-    for j in range(1, n_t):
-        if j != half:
-            entered((t + j < n_t) & (u + j >= half), j)
-    far_first = sorted(range(1, n_t), key=lambda j: abs(j - half))
-    for c in range(keep):
-        for kind in range(2):
-            own_mid(kind, c).wait()
-            for j in range(1, half):
-                source = within(half - j)
-                frame = source if kind == 0 else (source + half) % n_t
-                a2a(kind, c, j, within(j), frame).wait_recv()
-        for s in range(steps):
-            lo = s * chunk
-            span = max(1, block // chunk)
-
-            @pl.loop(0, n_t // span)
-            def _(i):
-                frames = pl.ds(i * span, span)
-                values = arrived[c, frames, lo : lo + chunk].astype(F32)
-                values = norm(values.reshape(span * chunk, width), tg[...])
-                where = pl.ds(pl.multiple_of(i * span * chunk, span * chunk), span * chunk)
-                normed_t[where] = values
-
-            if c == 0 and s == 0:
-                gathered(2)
-
-            @pl.loop(0, 3)
-            def _(i):
-                cols = pl.ds(pl.multiple_of(i * inner, LANES), inner)
-                part = jnp.dot(normed_t[...], wtq[:, cols], preferred_element_type=F32)
-                proj_t[:, :, cols] = part.reshape(n_t, chunk, inner)
-
-            for g in range(chunk // group):
-                at = g * group
-
-                def store(cols, result):
-                    ctx_t[c, :, lo + at : lo + at + group, cols] = result.reshape(
-                        n_t, group, LANES
-                    ).astype(BF16)
-
-                attend(
-                    lambda cols: proj_t[:, at : at + group, cols].reshape(size, LANES),
-                    size, same_place, store,
+    def place_of(s):
+        return side * (1 - core) + s * core, (2 * u + s) * (1 - core) + t * core
+
+    def own_back(s):
+        clip, slot = place_of(s)
+        return pltpu.make_async_copy(ctx_t.at[s, t], ctx_back.at[clip, slot], own_sem.at[2, s])
+
+    span = max(1, block // places)
+    for s in range(2):
+        arrive(s)
+
+        @pl.loop(0, n_t // span)
+        def _(i):
+            frames = pl.ds(i * span, span)
+            values = arrived[s, frames].astype(F32).reshape(span * places, width)
+            where = pl.ds(pl.multiple_of(i * span * places, span * places), span * places)
+            normed_t[where] = norm(values, tg[...])
+
+        if s == 0:
+            gathered(2)
+
+        @pl.loop(0, 3)
+        def _(i):
+            cols = pl.ds(pl.multiple_of(i * inner, LANES), inner)
+            part = jnp.dot(normed_t[...], wtq[:, cols], preferred_element_type=F32)
+            proj_t[:, :, cols] = part.reshape(n_t, places, inner)
+
+        for g in range(places // group):
+            at = g * group
+
+            def store(cols, result):
+                ctx_t[s, :, at : at + group, cols] = result.reshape(n_t, group, LANES).astype(
+                    BF16
                 )
-            for j in far_first:
-                start(back(c, s, j, (t + j) % n_t, side * keep + c, u))
-            own_back(c, s).start()
-    relay(3)
+
+            attend(
+                lambda cols: proj_t[:, at : at + group, cols].reshape(size, LANES),
+                size, same_place, store,
+            )
+        clip, slot = place_of(s)
+        for j in far_first:
+            back(s, j, (t + j) % n_t, clip, slot).start()
+        own_back(s).start()
+        if s == 0:
+            relay(3)
     gathered(3)
+    for cp in sends:
+        cp.wait_send()
+    for w in range(4):
+        mate_own(w, f).wait_send()
+
+    @pl.when(core == 0)
+    def _():
+        presend().wait_send()
+        near(0, drain)
+        near(1, drain)
+
+    @pl.when(core == 1)
+    def _():
+        wide(0, drain)
+        wide(1, drain)
 
     finals = []
-    for far in (False, True):
-        clip_side = 1 - side if far else side
-        for c in range(keep):
-            clip = clip_side * keep + c
-            job = (2 if far else 0) * keep + c
-            for s in range(steps):
-                lo = s * chunk
-                if not far:
-                    own_back(c, s).wait()
+    for e in range(2):
+        clip = first_clip if e == 0 else 1 - first_clip
+
+        @pl.when(core == 0)
+        def _():
+            for s in range(2):
+                if e == 0:
+                    own_back(s).wait()
                 for j in range(1, n_t):
                     source = (t + n_t - j) % n_t
 
-                    @pl.when((source // half == side) != far)
+                    @pl.when((source // half == side) == (e == 0))
                     def _():
-                        back(c, s, j, (t + j) % n_t, clip, source % half).wait_recv()
-
-                part_rows = half * chunk
-                now = ctx_back[clip, :, lo : lo + chunk].reshape(part_rows, inner)
-
-                @pl.loop(0, width // inner)
-                def _(i):
-                    cols = pl.ds(pl.multiple_of(i * inner, LANES), inner)
-                    base = mid[job, :, lo : lo + chunk, cols].astype(F32)
-                    part = base.reshape(part_rows, inner) + jnp.dot(
-                        now, wto[:, cols], preferred_element_type=F32
-                    )
-                    outv[far * keep + c, :, lo : lo + chunk, cols] = part.reshape(
-                        half, chunk, inner
-                    ).astype(BF16)
-
-            cp = pltpu.make_async_copy(outv.at[far * keep + c], out.at[clip], out_sem.at[far * keep + c])
-            cp.start()
-            finals.append(cp)
-
-    for c in range(keep):
-        presend(c).wait_send()
-        for kind in range(2):
-            for j in range(1, half):
-                a2a(kind, c, j, within(j), t).wait_send()
-    for w in range(4):
-        mate_own(w, f).wait_send()
-    for cp in sends:
-        cp.wait_send()
+                        back(s, j, source, source // half, 2 * (source % half) + s).wait_recv()
+
+        @pl.when(core == 1)
+        def _():
+            own_back(e).wait()
+            for j in range(1, n_t):
+                source = (t + n_t - j) % n_t
+                back(e, j, source, e, source).wait_recv()
+
+        now = ctx_back[clip]
+        if places % 16:
+            now = now.astype(F32)
+        ctx[...] = now.reshape(rows, inner).astype(BF16)
+
+        @pl.loop(0, width // inner)
+        def _(i):
+            cols = pl.ds(pl.multiple_of(i * inner, LANES), inner)
+            base = mid[2 * e, :, :, cols].astype(F32).reshape(rows, inner)
+            part = base + jnp.dot(ctx[...], wto[:, cols], preferred_element_type=F32)
+            outv[e, :, :, cols] = part.reshape(n_t, places, inner).astype(BF16)
+
+        cp = pltpu.make_async_copy(outv.at[e], out.at[clip], out_sem.at[e])
+        cp.start()
+        finals.append(cp)
+    for s in range(2):
+        for j in range(1, n_t):
+            back(s, j, (t + j) % n_t, 0, 0).wait_send()
     for cp in finals:
         cp.wait()
 
@@ -527,14 +556,11 @@
     temporal_out,
 ):
     clip_count, frames, rows, width = tokens.shape
-    assert frames == 1 and clip_count % 2 == 0 and n_t % 4 == 0
+    assert frames == 1 and clip_count == 2 and n_t % 4 == 0
     inner = spatial_out.shape[0] * n_f
     columns = spatial_qkv.shape[1]
-    keep = clip_count // 2
     half = n_t // 2
-    places = rows // half
-    steps = max(1, places // 32)
-    chunk = places // steps
+    places = rows // n_t
     peers = max(1, n_f // 2 - 1)
     most = pieces_of(max(spatial_qkv.shape[0], spatial_out.shape[0]))
     anywhere = pl.BlockSpec(memory_space=pl.ANY)
@@ -542,28 +568,28 @@
     dma = pltpu.SemaphoreType.DMA
     result = pl.pallas_call(
         functools.partial(kernel, n_f, n_t),
-        out_shape=jax.ShapeDtypeStruct((clip_count, half, places, width), BF16),
+        out_shape=jax.ShapeDtypeStruct((clip_count, n_t, places, width), BF16),
         in_specs=[anywhere, vmem, anywhere, anywhere, vmem, anywhere, anywhere],
         out_specs=anywhere,
         scratch_shapes=[
-            pltpu.VMEM((3 * keep, rows, width), BF16),
-            pltpu.VMEM((3 * keep, rows, width), BF16),
+            pltpu.VMEM((3, rows, width), BF16),
+            pltpu.VMEM((3, rows, width), BF16),
             pltpu.VMEM((rows, columns), F32),
             pltpu.VMEM((rows, inner), BF16),
-            pltpu.VMEM((3 * keep, half, places, width), BF16),
-            pltpu.VMEM((keep, n_t, places, width), BF16),
-            pltpu.VMEM((n_t * chunk, width), BF16),
-            pltpu.VMEM((n_t, chunk, columns), F32),
-            pltpu.VMEM((keep, n_t, places, inner), BF16),
-            pltpu.VMEM((clip_count, half, places, inner), BF16),
+            pltpu.VMEM((3, n_t, places, width), BF16),
+            pltpu.VMEM((2, n_t, places, width), BF16),
+            pltpu.VMEM((rows, width), BF16),
+            pltpu.VMEM((n_t, places, columns), F32),
+            pltpu.VMEM((2, n_t, places, inner), BF16),
+            pltpu.VMEM((2, n_t, places, inner), BF16),
             pltpu.VMEM((width, columns), BF16),
             pltpu.VMEM((inner, width), BF16),
             pltpu.VMEM((width, columns), BF16),
             pltpu.VMEM((inner, width), BF16),
-            pltpu.VMEM((clip_count, half, places, width), BF16),
+            pltpu.VMEM((2, n_t, places, width), BF16),
             pltpu.SemaphoreType.REGULAR((peers + 1,)),
             pltpu.SemaphoreType.REGULAR((n_t,)),
-            dma((3 * keep,)),
+            dma((3,)),
             dma((4,)),
             dma((4, peers, most)),
             dma((4, peers, most)),
@@ -573,14 +599,14 @@
             dma((4, peers, most)),
             dma((4,)),
             dma((4,)),
-            dma((keep,)),
-            dma((keep,)),
-            dma((2, keep, half)),
-            dma((2, keep, half)),
-            dma((keep, steps, n_t)),
-            dma((keep, steps, n_t)),
-            dma((2 + steps, keep)),
-            dma((clip_count,)),
+            dma,
+            dma,
+            dma((2, 2, n_t)),
+            dma((2, 2, n_t)),
+            dma((2, n_t)),
+            dma((2, n_t)),
+            dma((3, 2)),
+            dma((2,)),
         ],
         compiler_params=pltpu.CompilerParams(
             collective_id=0, has_side_effects=True, vmem_limit_bytes=67000000

time: 70.2 us -> 62.8 us (0.89)
  Pallas kernels: 67.7 us -> 60.4 us
    pallas_call x1, Pallas kernels: 67.7 us -> 60.4 us  [shards(): pl.pallas_call(functools.partial(kernel, n_f, n_t), out_shape=jax.ShapeDt...]
where the time goes in v2:
time: 62.8 us; the launch traced here: 62.6 us
  Pallas kernels  60.4 us (96%)
  local copies, waits for them, and re-layouts  2.26 us (4%)
    pallas_call x1, Pallas kernels, shards(): pl.pallas_call(functools.partial(kernel, n_f, n_t), out_shape=jax.ShapeDt...  60.4 us
    unnamed x1, local copies, waits for them, and re-layouts  2.26 us

profile of v2, /device:TPU:0, one launch (start us, length us, event | category | flops | bytes accessed | tf_op | source)
XLA Modules:
  0.0 62.6 jit_solution(8897805335963506713)
XLA Ops:
  0.0 60.4 %shard_map.73 = bf16[2,8,32,1024]{3,2,1,0:T(8,128)(2,1)} custom-call(bf16[2,256,1024]{2,1,0:T(8,128)(2,1)} %bitcast.7, f32[1,1024]{1,0:T(1,128)} %bitcast.8, bf16[256,1536]{1,0:T(8,128)(2,1)} %sqkv.1, bf16[128,1024]{1,0:T(8,128)(2,1)} %sout.1, f32[1,1024]{1,0:T(1,128)} %bitcast.9, bf16[256,1536]{1,0:T(8,128)(2,1)} %tqkv.1, bf16[128,1024]{1,0:T(8,128)(2,1)} %tout.1), custom_call_target="tpu_custom_call" | custom-call | tf_op jit(solution)/shard_map/pallas_call | solution.py:569
  60.4 2.3 %copy.10 = bf16[2,1,256,1024]{3,2,1,0:T(8,128)(2,1)} copy(bf16[2,1,256,1024]{3,2,1,0:T(8,128)(2,1)} %bitcast.6) | data formatting | bytes 2097152

commit v3 on v2

--- a/solution.py
+++ b/solution.py
@@ -400,8 +400,6 @@
     def _():
         wide(0, begin)
 
-    straight = counts(2)[0]
-    relay(2, 0, straight // 3)
 
     @pl.when(core == 0)
     def _():
@@ -419,14 +417,13 @@
     def _():
         wide(1, begin)
 
-    relay(2, straight // 3, 2 * straight // 3)
 
     @pl.when(core == 0)
     def _():
         spatial(2)
         spatial_out(2)
 
-    relay(2, 2 * straight // 3)
+    relay(2)
 
     group = min(places, max(8, LANES // n_t))
     size = n_t * group
@@ -487,8 +484,7 @@
         for j in far_first:
             back(s, j, (t + j) % n_t, clip, slot).start()
         own_back(s).start()
-        if s == 0:
-            relay(3)
+    relay(3)
     gathered(3)
     for cp in sends:
         cp.wait_send()

time: 62.8 us -> 62.8 us (level)
  no operation moved by 1% of the time
where the time goes in v3:
time: 62.8 us; the launch traced here: 62.6 us
  Pallas kernels  60.4 us (96%)
  local copies, waits for them, and re-layouts  2.26 us (4%)
    pallas_call x1, Pallas kernels, shards(): pl.pallas_call(functools.partial(kernel, n_f, n_t), out_shape=jax.ShapeDt...  60.4 us
    unnamed x1, local copies, waits for them, and re-layouts  2.26 us

profile of v3, /device:TPU:0, one launch (start us, length us, event | category | flops | bytes accessed | tf_op | source)
XLA Modules:
  0.0 62.6 jit_solution(4906340382497841215)
XLA Ops:
  0.0 60.4 %shard_map.73 = bf16[2,8,32,1024]{3,2,1,0:T(8,128)(2,1)} custom-call(bf16[2,256,1024]{2,1,0:T(8,128)(2,1)} %bitcast.7, f32[1,1024]{1,0:T(1,128)} %bitcast.8, bf16[256,1536]{1,0:T(8,128)(2,1)} %sqkv.1, bf16[128,1024]{1,0:T(8,128)(2,1)} %sout.1, f32[1,1024]{1,0:T(1,128)} %bitcast.9, bf16[256,1536]{1,0:T(8,128)(2,1)} %tqkv.1, bf16[128,1024]{1,0:T(8,128)(2,1)} %tout.1), custom_call_target="tpu_custom_call" | custom-call | tf_op jit(solution)/shard_map/pallas_call | solution.py:565
  60.4 2.3 %copy.10 = bf16[2,1,256,1024]{3,2,1,0:T(8,128)(2,1)} copy(bf16[2,1,256,1024]{3,2,1,0:T(8,128)(2,1)} %bitcast.6) | data formatting | bytes 2097152
